TPU v7x, 32 devices: a whole 2x2x4 slice. The times are simulated.
32 devices in a mesh: groups: 2 (over y), det: 4 (over z), blk: 2 (over x), sub: 2 (over core).
Axes of the slice: x: 2, y: 2, z: 4, core: 2. Of those that a mesh axis runs over, the one named last changes fastest.
Arguments:
- tod: float32 [256, 4, 1024], P(('groups', 'det'), None, ('blk', 'sub')), parts along dimension 0, may hold values from -30 to 30
- pixels: int32 [256, 4, 1024], P('groups', 'det', ('blk', 'sub')), parts along dimension 0, may hold values from 0 to 3071
- span_block: int32 [8, 8], P('groups', ('blk', 'sub')), parts along dimension 0, may hold values from 0 to 7
- weight_class: int32 [256], P('groups'), parts along dimension 0, may hold values from 0 to 7
- class_weight: float32 [16], P('groups'), parts along dimension 0, may hold values from 0.25 to 4
Outputs:
- signal_sum: float32 [16, 3072], P(('groups', 'blk'), ('det', 'sub')), parts along dimension 0
- weight_sum: float32 [16, 3072], P(('groups', 'blk'), ('det', 'sub')), parts along dimension 0
- hit_count: float32 [16, 3072], P(('groups', 'blk'), ('det', 'sub')), parts along dimension 0
There are 2 independent parts, one for each index of `groups`. A program takes and returns all parts, laid end to end along the dimension named above; each array names one. Nothing has to cross between parts.
All inputs are finite; a program needn't handle non-finite values.
Results may differ from a plain program's by a relative error of at most 0.005.
Values sent between devices are 32-bit elements; how exact they have to be, the bound alone decides.
A program may use at most 64 MiB of HBM per device.

v0:
```python
import jax
import jax.numpy as jnp
from jax import lax
from jax.sharding import PartitionSpec as P

BLOCK_PIX = 3072
SPAN = 128
BLK_OWN = 4


def on_device(tod, pixels, span_block, weight_class, class_weight):
    classes = class_weight.shape[0]
    picker = (weight_class[:, None] == jnp.arange(classes, dtype=jnp.int32)[None, :]).astype(
        jnp.float32
    )
    weight = jnp.sum(picker * class_weight[None, :], axis=1)
    total = jnp.sum(weight)
    regrouped = lax.all_to_all(tod, "det", split_axis=1, concat_axis=0, tiled=True)
    common = jnp.sum(weight[:, None, None] * regrouped, axis=0, keepdims=True) / total
    values = (weight[:, None, None] * (regrouped - common)).astype(jnp.bfloat16)
    detectors = values.shape[0]
    samples = values.shape[2]
    spans = samples // SPAN
    groups = 4
    size_group = detectors // groups
    turns = groups * spans
    own_row = lax.dynamic_slice_in_dim(span_block, lax.axis_index("det"), 1, 0)[0]
    values = (
        values.reshape(groups, size_group, spans, SPAN)
        .transpose(0, 2, 1, 3)
        .reshape(turns, size_group, SPAN)
    )
    where = (
        pixels.reshape(groups, size_group, spans, SPAN)
        .transpose(0, 2, 1, 3)
        .reshape(turns, size_group, SPAN)
    )
    weight_low = weight.astype(jnp.bfloat16).reshape(groups, 1, size_group)
    weight_low = jnp.broadcast_to(weight_low, (groups, spans, size_group)).reshape(
        turns, size_group
    )
    span_of = jnp.broadcast_to(
        jnp.arange(spans, dtype=jnp.int32)[None, :], (groups, spans)
    ).reshape(turns)
    lanes = 128
    upper = BLOCK_PIX // lanes
    nblocks = BLK_OWN * lax.axis_size("blk")
    count = size_group * SPAN
    selector = (span_of[:, None] == jnp.arange(spans, dtype=jnp.int32)[None, :]).astype(jnp.float32)

    def bin_tile(total_map, item):
        tile_values, tile_pixels, tile_weight, select = item
        high = tile_pixels // lanes
        low = tile_pixels % lanes
        high_hot = (high[..., None] == jnp.arange(upper, dtype=jnp.int32)).astype(jnp.bfloat16)
        first = tile_values[..., None] * high_hot
        second = tile_weight[:, None, None] * high_hot
        stacked = jnp.concatenate([first, second, high_hot], axis=-1).reshape(count, 3 * upper)
        low_hot = (
            (low[..., None] == jnp.arange(lanes, dtype=jnp.int32))
            .astype(jnp.bfloat16)
            .reshape(count, lanes)
        )
        binned = lax.dot_general(
            stacked, low_hot, (((0,), (0,)), ((), ())), preferred_element_type=jnp.float32
        )
        return (total_map + select[:, None, None] * binned[None], None)

    start = jnp.zeros((spans, 3 * upper, lanes), jnp.float32)
    binned_map, unused = lax.scan(bin_tile, start, (values, where, weight_low, selector))
    binned_map = binned_map.reshape(spans, 3, BLOCK_PIX)
    count_det = lax.axis_size("det")
    count_sub = lax.axis_size("sub")
    peers = count_det * count_sub
    width = BLOCK_PIX // peers
    pieces = binned_map.reshape(spans, 3, peers, width)
    labels = jnp.broadcast_to(
        own_row.astype(jnp.float32)[:, None, None, None], (spans, 1, peers, 1)
    )
    received, got_labels = (
        lax.all_to_all(pieces, ("det", "sub"), split_axis=2, concat_axis=0, tiled=True),
        lax.all_to_all(labels, ("det", "sub"), split_axis=2, concat_axis=0, tiled=True),
    )
    received = received.reshape(peers * spans, 3 * width)
    got_labels = got_labels.reshape(peers * spans)
    placing = (got_labels[:, None] == jnp.arange(nblocks, dtype=jnp.float32)[None, :]).astype(
        jnp.float32
    )
    gathered = lax.dot_general(
        placing,
        received,
        (((0,), (0,)), ((), ())),
        precision=lax.Precision.HIGHEST,
        preferred_element_type=jnp.float32,
    )
    gathered = gathered.reshape(nblocks, 3, width)
    mine = lax.psum_scatter(gathered, "blk", scatter_dimension=0, tiled=True)
    signal_sum, weight_sum, hit_count = (mine[:, 0], mine[:, 1], mine[:, 2])
    return (signal_sum, weight_sum, hit_count)


def solution(mesh):
    placed = (
        P(("groups", "det"), None, ("blk", "sub")),
        P("groups", "det", ("blk", "sub")),
        P("groups", ("blk", "sub")),
        P("groups"),
        P("groups"),
    )
    return jax.shard_map(
        on_device,
        mesh=mesh,
        in_specs=placed,
        out_specs=(
            P(("groups", "blk"), ("det", "sub")),
            P(("groups", "blk"), ("det", "sub")),
            P(("groups", "blk"), ("det", "sub")),
        ),
        check_vma=False,
    )
```

profile of v0, /device:TPU:0, one launch (start us, length us, event | category | flops | bytes accessed | tf_op | source)
XLA Modules:
  0.0 50.1 jit_solution(9082960590155810975)
XLA Ops:
  0.6 1.6 %copy.35 = f32[32,4,256]{2,0,1:T(8,128)} copy(f32[32,4,256]{2,1,0:T(4,128)} %param.7) | data formatting | bytes 262144 | tf_op args[0]
  2.2 0.0 copy-start.2
  2.2 0.0 copy-start.3
  2.2 0.0 copy-start
  2.2 6.5 %all-to-all-start.1 = ((f32[32,4,256]{2,0,1:T(8,128)}), f32[32,4,256]{2,0,1:T(8,128)S(1)}, u32[]{:S(2)}, u32[]{:S(2)}) async-start(f32[32,4,256]{2,0,1:T(8,128)} %copy.35), calls=%async_computation.1 | async-start | bytes 262144 | tf_op jit(solution)/shard_map/all_to_all | solution.py:18
  8.7 0.0 copy-start.1
  8.7 0.0 copy-done.2
  8.7 0.0 copy-done.3
  8.7 0.7 %select_reduce_fusion = (f32[]{:T(128)}, f32[128]{0:T(128)S(1)}) fusion(f32[8]{0:T(128)S(1)} %copy-done.2, s32[128]{0:T(128)S(1)} %copy-done.3), kind=kLoop, calls=%fused_computation.40 | loop fusion | flops 3967 | bytes 1060 | tf_op jit(solution)/shard_map/reduce_sum | solution.py:17
  9.4 0.1 mul.98
  9.5 0.0 copy-done
  9.5 0.1 eq.91
  9.6 0.0 copy-done.1
  9.6 0.2 convert_reduce_fusion
  9.8 0.1 fusion.24
  9.8 4.9 %all-to-all-done.1 = f32[32,4,256]{2,0,1:T(8,128)S(1)} async-done(((f32[32,4,256]{2,0,1:T(8,128)}), f32[32,4,256]{2,0,1:T(8,128)S(1)}, u32[]{:S(2)}, u32[]{:S(2)}) %all-to-all-start.1) | async-done | bytes 131104 | tf_op jit(solution)/shard_map/all_to_all | solution.py:18
  14.8 0.6 %broadcast_in_dim.8 = f32[2,1,8,1]{0,3,1,2:T(1,128)} broadcast(f32[2]{0:T(128)S(1)} %convert_reduce_fusion), dimensions={0} | broadcast | bytes 72 | tf_op jit(solution)/shard_map/broadcast_in_dim | solution.py:77
  15.3 3.3 %all-to-all-start = ((f32[2,1,8,1]{0,3,1,2:T(1,128)}), f32[2,1,8,1]{0,3,1,2:T(1,128)S(1)}, u32[]{:S(2)}, u32[]{:S(2)}) async-start(f32[2,1,8,1]{0,3,1,2:T(1,128)} %broadcast_in_dim.8), calls=%async_computation | async-start | bytes 8192 | tf_op jit(solution)/shard_map/all_to_all | solution.py:82
  18.7 0.1 fusion.17
  18.8 0.1 all_to_all.43
  18.8 0.7 %divide_bitcast_fusion = f32[2,128]{1,0:T(2,128)S(1)} fusion(f32[256]{0:T(256)S(1)} %fusion.17, f32[]{:T(128)} %get-tuple-element.105), kind=kLoop, calls=%fused_computation.48 | loop fusion | flops 256 | bytes 2052 | tf_op jit(solution)/shard_map/div | solution.py:19
  19.5 0.2 fusion.21
  19.7 9.3 %while.13 = (s32[]{:T(128)}, f32[2,72,128]{2,1,0:T(8,128)S(1)}, f32[8,2]{1,0:T(8,128)S(1)}, s32[8,32,128]{2,1,0:T(8,128)S(1)}, bf16[8,32,128]{2,1,0:T(8,128)(2,1...) while((s32[]{:T(128)}, f32[2,72,128]{2,1,0:T(8,128)S(1)}, f32[8,2]{1,0:T(8,128)S(1)}, ...), condition=%wide.region_4.5_spmd.clone, body=%wide.region_3.4_spmd.clone.sunk | while | flops 78440448 | bytes 1548619 | solution.py:70
  19.8 0.1 fusion.35
  20.0 0.8 %fusion.36 = f32[72,128]{1,0:T(8,128)S(1)} fusion(s32[32,128]{1,0:T(8,128)S(1)} %add_select_fusion.5, bf16[32,128,24]{1,2,0:T(8,128)(2,1)S(1)} %fusion.33, bf16[32,128,24]{1,2,0:T(8,128)(2,1)S(1)} %get-tuple-element.169, bf16[32,128,24]{1,2,0:T(8,128)(2,1)S(1)} %get-tuple-element.170), kind=kOutput, calls=%fused_computation.2.clone.1 | convolution fusion | flops 77791232 | bytes 643072 | tf_op jit(solution)/shard_map/while/body/eval_jaxpr/dot_general | solution.py:64
  20.8 0.1 select_add_fusion.2
  21.0 0.1 fusion.35
  21.2 0.8 %fusion.36 = f32[72,128]{1,0:T(8,128)S(1)} fusion(s32[32,128]{1,0:T(8,128)S(1)} %add_select_fusion.5, bf16[32,128,24]{1,2,0:T(8,128)(2,1)S(1)} %fusion.33, bf16[32,128,24]{1,2,0:T(8,128)(2,1)S(1)} %get-tuple-element.169, bf16[32,128,24]{1,2,0:T(8,128)(2,1)S(1)} %get-tuple-element.170), kind=kOutput, calls=%fused_computation.2.clone.1 | convolution fusion | flops 77791232 | bytes 643072 | tf_op jit(solution)/shard_map/while/body/eval_jaxpr/dot_general | solution.py:64
  22.0 0.1 select_add_fusion.2
  22.1 0.1 fusion.35
  22.3 0.8 %fusion.36 = f32[72,128]{1,0:T(8,128)S(1)} fusion(s32[32,128]{1,0:T(8,128)S(1)} %add_select_fusion.5, bf16[32,128,24]{1,2,0:T(8,128)(2,1)S(1)} %fusion.33, bf16[32,128,24]{1,2,0:T(8,128)(2,1)S(1)} %get-tuple-element.169, bf16[32,128,24]{1,2,0:T(8,128)(2,1)S(1)} %get-tuple-element.170), kind=kOutput, calls=%fused_computation.2.clone.1 | convolution fusion | flops 77791232 | bytes 643072 | tf_op jit(solution)/shard_map/while/body/eval_jaxpr/dot_general | solution.py:64
  23.1 0.1 select_add_fusion.2
  23.3 0.1 fusion.35
  23.5 0.8 %fusion.36 = f32[72,128]{1,0:T(8,128)S(1)} fusion(s32[32,128]{1,0:T(8,128)S(1)} %add_select_fusion.5, bf16[32,128,24]{1,2,0:T(8,128)(2,1)S(1)} %fusion.33, bf16[32,128,24]{1,2,0:T(8,128)(2,1)S(1)} %get-tuple-element.169, bf16[32,128,24]{1,2,0:T(8,128)(2,1)S(1)} %get-tuple-element.170), kind=kOutput, calls=%fused_computation.2.clone.1 | convolution fusion | flops 77791232 | bytes 643072 | tf_op jit(solution)/shard_map/while/body/eval_jaxpr/dot_general | solution.py:64
  24.3 0.1 select_add_fusion.2
  24.4 0.1 fusion.35
  24.6 0.8 %fusion.36 = f32[72,128]{1,0:T(8,128)S(1)} fusion(s32[32,128]{1,0:T(8,128)S(1)} %add_select_fusion.5, bf16[32,128,24]{1,2,0:T(8,128)(2,1)S(1)} %fusion.33, bf16[32,128,24]{1,2,0:T(8,128)(2,1)S(1)} %get-tuple-element.169, bf16[32,128,24]{1,2,0:T(8,128)(2,1)S(1)} %get-tuple-element.170), kind=kOutput, calls=%fused_computation.2.clone.1 | convolution fusion | flops 77791232 | bytes 643072 | tf_op jit(solution)/shard_map/while/body/eval_jaxpr/dot_general | solution.py:64
  25.5 0.1 select_add_fusion.2
  25.6 0.1 fusion.35
  25.8 0.8 %fusion.36 = f32[72,128]{1,0:T(8,128)S(1)} fusion(s32[32,128]{1,0:T(8,128)S(1)} %add_select_fusion.5, bf16[32,128,24]{1,2,0:T(8,128)(2,1)S(1)} %fusion.33, bf16[32,128,24]{1,2,0:T(8,128)(2,1)S(1)} %get-tuple-element.169, bf16[32,128,24]{1,2,0:T(8,128)(2,1)S(1)} %get-tuple-element.170), kind=kOutput, calls=%fused_computation.2.clone.1 | convolution fusion | flops 77791232 | bytes 643072 | tf_op jit(solution)/shard_map/while/body/eval_jaxpr/dot_general | solution.py:64
  26.6 0.1 select_add_fusion.2
  26.7 0.1 fusion.35
  26.9 0.8 %fusion.36 = f32[72,128]{1,0:T(8,128)S(1)} fusion(s32[32,128]{1,0:T(8,128)S(1)} %add_select_fusion.5, bf16[32,128,24]{1,2,0:T(8,128)(2,1)S(1)} %fusion.33, bf16[32,128,24]{1,2,0:T(8,128)(2,1)S(1)} %get-tuple-element.169, bf16[32,128,24]{1,2,0:T(8,128)(2,1)S(1)} %get-tuple-element.170), kind=kOutput, calls=%fused_computation.2.clone.1 | convolution fusion | flops 77791232 | bytes 643072 | tf_op jit(solution)/shard_map/while/body/eval_jaxpr/dot_general | solution.py:64
  27.8 0.1 select_add_fusion.2
  27.9 0.1 fusion.35
  28.1 0.8 %fusion.36 = f32[72,128]{1,0:T(8,128)S(1)} fusion(s32[32,128]{1,0:T(8,128)S(1)} %add_select_fusion.5, bf16[32,128,24]{1,2,0:T(8,128)(2,1)S(1)} %fusion.33, bf16[32,128,24]{1,2,0:T(8,128)(2,1)S(1)} %get-tuple-element.169, bf16[32,128,24]{1,2,0:T(8,128)(2,1)S(1)} %get-tuple-element.170), kind=kOutput, calls=%fused_computation.2.clone.1 | convolution fusion | flops 77791232 | bytes 643072 | tf_op jit(solution)/shard_map/while/body/eval_jaxpr/dot_general | solution.py:64
  28.9 0.1 select_add_fusion.2
  29.0 0.0 copy-start.4
  29.0 0.7 %copy.37 = f32[2,3,8,384]{3,0,1,2:T(2,128)} copy(f32[2,3,8,384]{3,2,1,0:T(8,128)S(1)} %reshape_reshape.3) | data formatting | bytes 147456 | tf_op jit(solution)/shard_map/reshape;reshape | solution.py:76
  29.7 0.0 all-to-all-done
  29.7 5.0 %all-to-all-start.2 = ((f32[2,3,8,384]{3,0,1,2:T(2,128)}), f32[2,3,8,384]{3,0,1,2:T(2,128)S(1)}, u32[]{:S(2)}, u32[]{:S(2)}) async-start(f32[2,3,8,384]{3,0,1,2:T(2,128)} %copy.37), calls=%async_computation.2 | async-start | bytes 147456 | tf_op jit(solution)/shard_map/all_to_all | solution.py:81
  34.7 0.0 copy-done.4
  34.7 0.6 %dynamic-slice = u32[1]{0:T(128)} dynamic-slice(u32[32]{0:T(128)S(1)} %copy-done.4, u32[]{:T(128)S(6)} %add.43), dynamic_slice_sizes={1} | dynamic-slice | bytes 12
  36.0 0.1 copy.32
  36.0 0.1 copy.33
  36.1 0.1 eq.87
  36.2 4.5 %all-to-all-done.2 = f32[2,3,8,384]{3,0,1,2:T(2,128)S(1)} async-done(((f32[2,3,8,384]{3,0,1,2:T(2,128)}), f32[2,3,8,384]{3,0,1,2:T(2,128)S(1)}, u32[]{:S(2)}, u32[]{:S(2)}) %all-to-all-start.2) | async-done | bytes 73760 | tf_op jit(solution)/shard_map/all_to_all | solution.py:81
  40.7 0.1 fusion.18
  40.9 8.6 %all-reduce = f32[8,3,384]{2,0,1:T(8,128)S(1)} all-reduce(f32[8,3,384]{2,0,1:T(8,128)S(1)} %fusion.18), channel_id=2, replica_groups=mesh['groups'=2,'det'=4,'blk'=2,'sub'=2] {'blk'}, use_global_device_ids=true, to_apply=%region_5.6.clone | all-reduce | flops 9216 | bytes 73728
  49.5 0.6 %dynamic-slice_bitcast_fusion.1 = (f32[4,384]{1,0:T(4,128)}, f32[4,384]{1,0:T(4,128)}, f32[4,384]{1,0:T(4,128)}) fusion(f32[8,3,384]{2,0,1:T(8,128)S(1)} %all-reduce, u32[]{:T(128)S(6)} %multiply.1, u32[]{:T(128)S(6)} %convert.1, u32[]{:T(128)S(6)} %convert), kind=kLoop, calls=%fused_computation.37 | loop fusion | bytes 36876 | tf_op jit(solution)/shard_map/squeeze | solution.py:98
  (56 shorter events, 1.0 us)
Async XLA Ops:
  2.2 6.5 %copy-start.2 = (f32[8]{0:T(128)S(1)}, f32[8]{0:T(128)}, u32[]{:S(2)}) copy-start(f32[8]{0:T(128)} %param.11) | copy-start | bytes 100
  2.2 6.5 %copy-start.3 = (s32[128]{0:T(128)S(1)}, s32[128]{0:T(128)}, u32[]{:S(2)}) copy-start(s32[128]{0:T(128)} %param.10) | copy-start | bytes 1540
  2.2 7.3 %copy-start = (s32[128,1,256]{2,1,0:T(1,128)S(1)}, s32[128,1,256]{2,1,0:T(1,128)}, u32[]{:S(2)}) copy-start(s32[128,1,256]{2,1,0:T(1,128)} %param.8) | copy-start | bytes 393220
  2.2 12.6 %all-to-all-start.1 = ((f32[32,4,256]{2,0,1:T(8,128)}), f32[32,4,256]{2,0,1:T(8,128)S(1)}, u32[]{:S(2)}, u32[]{:S(2)}) async-start(f32[32,4,256]{2,0,1:T(8,128)} %copy.35), calls=%async_computation.1 | async-start | bytes 262144 | tf_op jit(solution)/shard_map/all_to_all | solution.py:18
  8.7 0.9 %copy-start.1 = (s32[4,2]{0,1:T(2,128)S(1)}, s32[4,2]{0,1:T(2,128)}, u32[]{:S(2)}) copy-start(s32[4,2]{0,1:T(2,128)} %param.9) | copy-start | bytes 100
  15.3 14.3 %all-to-all-start = ((f32[2,1,8,1]{0,3,1,2:T(1,128)}), f32[2,1,8,1]{0,3,1,2:T(1,128)S(1)}, u32[]{:S(2)}, u32[]{:S(2)}) async-start(f32[2,1,8,1]{0,3,1,2:T(1,128)} %broadcast_in_dim.8), calls=%async_computation | async-start | bytes 8192 | tf_op jit(solution)/shard_map/all_to_all | solution.py:82
  29.0 5.7 %copy-start.4 = (u32[32]{0:T(128)S(1)}, u32[32]{0:T(128)}, u32[]{:S(2)}) copy-start(u32[32]{0:T(128)} %constant.84) | copy-start | bytes 388
  29.7 11.0 %all-to-all-start.2 = ((f32[2,3,8,384]{3,0,1,2:T(2,128)}), f32[2,3,8,384]{3,0,1,2:T(2,128)S(1)}, u32[]{:S(2)}, u32[]{:S(2)}) async-start(f32[2,3,8,384]{3,0,1,2:T(2,128)} %copy.37), calls=%async_computation.2 | async-start | bytes 147456 | tf_op jit(solution)/shard_map/all_to_all | solution.py:81
where the time goes:
time: 50.5 us; the launch traced here: 50.1 us
  starting transfers between devices  14.8 us (29%)
  waiting for transfers between devices  9.42 us (19%)
  blocking collectives  8.57 us (17%)
  matrix products  6.57 us (13%)
  local copies, waits for them, and re-layouts  4.85 us (10%)
  other arithmetic  4.02 us (8%)
  between operations  1.39 us (3%)
    unnamed x1, blocking collectives  8.57 us
    all_to_all x1, starting transfers between devices, on_device(): lax.all_to_all(tod, 'det', split_axis=1, concat_axis=0, tiled=True)  6.48 us
    dot_general x8, matrix products, bin_tile(): lax.dot_general(stacked, low_hot, (((0,), (0,)), ((), ())), preferred_ele...  6.42 us
    all_to_all x1, starting transfers between devices, on_device(): lax.all_to_all(pieces, ('det', 'sub'), split_axis=2, concat_axis=0, tiled...  5.03 us
    all_to_all x1, waiting for transfers between devices, on_device(): lax.all_to_all(tod, 'det', split_axis=1, concat_axis=0, tiled=True)  4.93 us
    all_to_all x1, waiting for transfers between devices, on_device(): lax.all_to_all(pieces, ('det', 'sub'), split_axis=2, concat_axis=0, tiled...  4.49 us
    all_to_all x1, starting transfers between devices, on_device(): lax.all_to_all(labels, ('det', 'sub'), split_axis=2, concat_axis=0, tiled...  3.31 us
    unnamed x12, local copies, waits for them, and re-layouts  2.17 us
  transfers between devices with their start and end apart: 3, of which 2 were waited for; matrix products, arithmetic and copies ran while one was open for 25% of the time, Pallas kernels for 0%

commit v1 on v0

v1 whole, which is shorter than its diff:
```python
import functools

import jax
import jax.numpy as jnp
from jax import lax
from jax.experimental import pallas as pl
from jax.experimental.pallas import tpu as pltpu
from jax.sharding import PartitionSpec as P

BLOCK_PIX = 3072
SPAN = 128
BLK_OWN = 4
TILE = 8
PACK = 16
MESH = pl.DeviceIdType.MESH


def kernel(
    sizes,
    tod_hbm,
    pix_hbm,
    class_ref,
    class_weight_ref,
    span_block_ref,
    signal_ref,
    weight_ref,
    hits_ref,
    tod_in,
    pix_in,
    stage,
    tod_all,
    high_ref,
    low_ref,
    weight_rows,
    value_ref,
    early_out,
    early_in,
    late_out,
    late_in,
    load_sem,
    tod_send,
    tod_recv,
    early_send,
    early_recv,
    late_send,
    late_recv,
):
    ndet, nblk, nsub, spans, lanes, rows = sizes
    peers = ndet * nsub
    total_peers = peers * nblk
    mine = tod_hbm.shape[0]
    detectors = ndet * mine
    classes = class_weight_ref.shape[0]
    det = lax.axis_index("det")
    blk = lax.axis_index("blk")
    sub = lax.axis_index("sub")
    load_tod = pltpu.make_async_copy(tod_hbm, tod_in, load_sem.at[0])
    load_pix = pltpu.make_async_copy(pix_hbm, pix_in, load_sem.at[1])
    load_tod.start()
    load_pix.start()
    others = [
        (db, dd, ds)
        for dd in range(ndet)
        for db in range(nblk)
        for ds in range(nsub)
        if (db, dd, ds) != (0, 0, 0)
    ]

    def target(offset):
        db, dd, ds = offset
        return {
            "det": lax.rem(det + dd, ndet),
            "blk": lax.rem(blk + db, nblk),
            "sub": lax.rem(sub + ds, nsub),
        }

    barrier = pltpu.get_barrier_semaphore()
    for offset in others:
        pl.semaphore_signal(barrier, inc=1, device_id=target(offset), device_id_type=MESH)

    part = mine * spans
    load_tod.wait()
    for seg in range(ndet):
        for span in range(spans):
            stage[seg, pl.ds(span, mine, spans), :] = tod_in[:, seg, span * SPAN : (span + 1) * SPAN]
    pl.semaphore_wait(barrier, len(others))
    for step in range(1, ndet):
        seg = lax.rem(det + step, ndet)
        pltpu.make_async_remote_copy(
            src_ref=stage.at[seg],
            dst_ref=tod_all.at[det],
            send_sem=tod_send,
            recv_sem=tod_recv,
            device_id={"det": seg},
            device_id_type=MESH,
        ).start()
    tod_all[det] = stage[det]

    picked = jnp.zeros((1, detectors), jnp.float32)
    for c in range(classes):
        picked = jnp.where(class_ref[...] == c, class_weight_ref[c], picked)
    total = jnp.sum(picked, axis=1, keepdims=True)
    turned = jnp.transpose(jnp.broadcast_to(picked, (SPAN, detectors)))
    for span in range(spans):
        weight_rows[pl.ds(span, detectors, spans), :] = turned

    load_pix.wait()
    pixel = pix_in[...].astype(jnp.float32)
    high = jnp.floor((pixel + 0.5) * (1.0 / lanes))
    high_ref[...] = high
    low_ref[...] = pixel - high * lanes

    height = peers * TILE
    low_tiles = -(-lanes // PACK)

    def iota(tile):
        return lax.broadcasted_iota(jnp.int32, (PACK, SPAN), 0) + tile * PACK

    def to_low(x):
        return x.astype(jnp.float32).astype(jnp.bfloat16)

    low_ids = [to_low(iota(t)) for t in range(SPAN // PACK)]
    early_ids = []
    late_ids = [[] for _ in range(spans)]
    for t in range(height // PACK):
        row = iota(t)
        peer = row // TILE
        within = row % TILE
        kind = jnp.where(within < rows, within, within - rows)
        early_ids.append(to_low(jnp.where(within < 2 * rows, peer * rows + kind, -1)))
        for span in range(spans):
            inner = within - span * rows
            valid = jnp.logical_and(inner >= 0, inner < rows)
            late_ids[span].append(to_low(jnp.where(valid, peer * rows + inner, -1)))
    is_weight = to_low(jnp.where(iota(0) % TILE < rows, 1, 0)) > 0.5
    one = jnp.ones((PACK, SPAN), jnp.bfloat16)
    zero = jnp.zeros((PACK, SPAN), jnp.bfloat16)

    def spread(ref, row):
        return jnp.broadcast_to(ref[pl.ds(row, 1), :], (PACK, SPAN)).astype(jnp.bfloat16)

    def hot(ids, where, filled):
        return jnp.concatenate([jnp.where(i == where, filled, zero) for i in ids], axis=0)

    chunk = 8

    def contract(left, right):
        return lax.dot_general(
            jnp.concatenate(left, axis=1),
            jnp.concatenate(right, axis=1),
            (((1,), (1,)), ((), ())),
            preferred_element_type=jnp.float32,
        )

    def early_step(i, sums):
        base = pl.multiple_of(i * chunk * spans, TILE)
        new = []
        for span in range(spans):
            left, right = [], []
            for d in range(chunk):
                r = base + d * spans + span
                right.append(hot(low_ids, spread(low_ref, r), one))
                filled = jnp.where(is_weight, spread(weight_rows, r), one)
                left.append(hot(early_ids, spread(high_ref, r), filled))
            new.append(sums[span] + contract(left, right))
        return tuple(new)

    start = tuple(jnp.zeros((height, SPAN), jnp.float32) for _ in range(spans))
    sums = lax.fori_loop(0, detectors // chunk, early_step, start)
    label_row = lax.broadcasted_iota(jnp.int32, (TILE, SPAN), 0) == 2 * rows
    for span in range(spans):
        label = span_block_ref[det, span].astype(jnp.float32)
        for p in range(peers):
            tile = sums[span][p * TILE : (p + 1) * TILE]
            early_out[p, span] = jnp.where(label_row, label, tile)

    slot_of = {offset: n for n, offset in enumerate(others)}

    def send(source, landing, send_sem, recv_sem):
        for offset in others:
            to = target(offset)
            pltpu.make_async_remote_copy(
                src_ref=source.at[to["det"] * nsub + to["sub"]],
                dst_ref=landing.at[slot_of[offset]],
                send_sem=send_sem,
                recv_sem=recv_sem,
                device_id=to,
                device_id_type=MESH,
            ).start()

    own_place = det * nsub + sub
    remote = len(others)

    tod_gone = stage.at[pl.ds(0, ndet - 1)]
    pltpu.make_async_copy(tod_gone, tod_all.at[pl.ds(0, ndet - 1)], tod_recv).wait()
    send(early_out, early_in, early_send, early_recv)

    period = TILE
    folded = jnp.zeros((period, SPAN), jnp.float32)
    for q in range(ndet):
        weighted = tod_all[q] * weight_rows[q * part : (q + 1) * part]
        for k in range(part // period):
            folded = folded + weighted[k * period : (k + 1) * period]
    shift = spans
    while shift < period:
        folded = folded + pltpu.roll(folded, shift, 0)
        shift *= 2
    common = folded / total
    for q in range(ndet):
        piece = slice(q * part, (q + 1) * part)
        repeated = jnp.concatenate([common] * (part // period), axis=0)
        value_ref[piece] = weight_rows[piece] * (tod_all[q] - repeated)

    def late_step(i, total_sum):
        base = pl.multiple_of(i * chunk * spans, TILE)
        for span in range(spans):
            left, right = [], []
            for d in range(chunk):
                r = base + d * spans + span
                right.append(hot(low_ids, spread(low_ref, r), one))
                left.append(hot(late_ids[span], spread(high_ref, r), spread(value_ref, r)))
            total_sum = total_sum + contract(left, right)
        return total_sum

    late = lax.fori_loop(0, detectors // chunk, late_step, jnp.zeros((height, SPAN), jnp.float32))
    for p in range(peers):
        late_out[p] = late[p * TILE : (p + 1) * TILE]
    send(late_out, late_in, late_send, late_recv)
    late_in[remote] = late_out[own_place]
    early_in[remote] = early_out[own_place]

    pltpu.make_async_copy(early_in.at[pl.ds(0, remote)], early_in.at[pl.ds(0, remote)], early_recv).wait()
    first = (blk * BLK_OWN).astype(jnp.float32)

    def gather_early(n, acc):
        acc = list(acc)
        for span in range(spans):
            tile = early_in[n, span]
            label = jnp.broadcast_to(early_in[n, span, pl.ds(2 * rows, 1), :], (TILE, SPAN))
            for b in range(BLK_OWN):
                acc[b] = acc[b] + jnp.where(label == first + b, tile, 0.0)
        return tuple(acc)

    within = lax.broadcasted_iota(jnp.int32, (TILE, SPAN), 0)

    def gather_late(n, acc):
        label = jnp.broadcast_to(early_in[n, 0, pl.ds(2 * rows, 1), :], (TILE, SPAN))
        for span in range(1, spans):
            other = jnp.broadcast_to(early_in[n, span, pl.ds(2 * rows, 1), :], (TILE, SPAN))
            label = jnp.where(within < span * rows, label, other)
        tile = late_in[n]
        return tuple(
            acc[b] + jnp.where(label == first + b, tile, 0.0) for b in range(BLK_OWN)
        )

    def over_slots(step):
        acc = tuple(jnp.zeros((TILE, SPAN), jnp.float32) for _ in range(BLK_OWN))
        if total_peers <= 16:
            for n in range(total_peers):
                acc = step(n, acc)
            return acc
        return lax.fori_loop(0, total_peers, step, acc)

    acc = over_slots(gather_early)
    for b in range(BLK_OWN):
        for r in range(rows):
            at = slice(r * lanes, (r + 1) * lanes)
            weight_ref[b : b + 1, at] = acc[b][r : r + 1, :lanes]
            hits_ref[b : b + 1, at] = acc[b][rows + r : rows + r + 1, :lanes]

    pltpu.make_async_copy(late_in.at[pl.ds(0, remote)], late_in.at[pl.ds(0, remote)], late_recv).wait()
    acc = over_slots(gather_late)
    for b in range(BLK_OWN):
        for r in range(rows):
            line = acc[b][r : r + 1]
            for span in range(1, spans):
                line = line + acc[b][span * rows + r : span * rows + r + 1]
            signal_ref[b : b + 1, r * lanes : (r + 1) * lanes] = line[:, :lanes]

    pltpu.make_async_copy(tod_gone, tod_all.at[pl.ds(0, ndet - 1)], tod_send).wait()
    pltpu.make_async_copy(early_in.at[pl.ds(0, remote)], early_in.at[pl.ds(0, remote)], early_send).wait()
    pltpu.make_async_copy(late_in.at[pl.ds(0, remote)], late_in.at[pl.ds(0, remote)], late_send).wait()


def on_device(tod, pixels, span_block, weight_class, class_weight):
    ndet, nblk, nsub = (lax.axis_size(a) for a in ("det", "blk", "sub"))
    mine, segments, samples = tod.shape
    detectors = pixels.shape[0]
    spans = samples // SPAN
    peers = ndet * nsub
    slots = peers * nblk
    width = BLOCK_PIX // peers
    lanes = next(n for n in range(SPAN, 0, -1) if width % n == 0)
    rows = width // lanes
    assert segments == ndet and detectors == ndet * mine
    assert TILE % spans == 0 and rows * spans <= TILE and 2 * rows < TILE
    flat = (detectors * spans, SPAN)
    out = jax.ShapeDtypeStruct((BLK_OWN, width), jnp.float32)
    vmem = pl.BlockSpec(memory_space=pltpu.VMEM)
    smem = pl.BlockSpec(memory_space=pltpu.SMEM)
    hbm = pl.BlockSpec(memory_space=pl.ANY)
    f32 = jnp.float32
    dma = pltpu.SemaphoreType.DMA
    return pl.pallas_call(
        functools.partial(kernel, (ndet, nblk, nsub, spans, lanes, rows)),
        out_shape=(out, out, out),
        in_specs=[hbm, hbm, vmem, smem, smem],
        out_specs=(vmem, vmem, vmem),
        scratch_shapes=[
            pltpu.VMEM(tod.shape, f32),
            pltpu.VMEM(flat, jnp.int32),
            pltpu.VMEM((ndet, mine * spans, SPAN), f32),
            pltpu.VMEM((ndet, mine * spans, SPAN), f32),
            pltpu.VMEM(flat, f32),
            pltpu.VMEM(flat, f32),
            pltpu.VMEM(flat, f32),
            pltpu.VMEM(flat, f32),
            pltpu.VMEM((peers, spans, TILE, SPAN), f32),
            pltpu.VMEM((slots, spans, TILE, SPAN), f32),
            pltpu.VMEM((peers, TILE, SPAN), f32),
            pltpu.VMEM((slots, TILE, SPAN), f32),
            dma((2,)),
            dma,
            dma,
            dma,
            dma,
            dma,
            dma,
        ],
        compiler_params=pltpu.CompilerParams(collective_id=0, has_side_effects=True),
    )(
        tod,
        pixels.reshape(flat),
        weight_class.reshape(1, detectors),
        class_weight,
        span_block,
    )


def solution(mesh):
    placed = (
        P(("groups", "det"), None, ("blk", "sub")),
        P("groups", "det", ("blk", "sub")),
        P("groups", ("blk", "sub")),
        P("groups"),
        P("groups"),
    )
    sliced = P(("groups", "blk"), ("det", "sub"))
    return jax.shard_map(
        on_device,
        mesh=mesh,
        in_specs=placed,
        out_specs=(sliced, sliced, sliced),
        check_vma=False,
    )
```

time: 50.5 us -> 25.9 us (0.51)
  Pallas kernels: 0 us -> 21.1 us
  starting transfers between devices: 14.8 us -> 0 us
  waiting for transfers between devices: 9.42 us -> 0 us
  blocking collectives: 8.57 us -> 0 us
  matrix products: 6.57 us -> 0 us
  other arithmetic: 4.02 us -> 0 us
  local copies, waits for them, and re-layouts: 4.85 us -> 3.92 us
  between operations: 1.39 us -> 0.66 us
    pallas_call x0 -> x1, Pallas kernels: none -> 21.1 us  [on_device(): pl.pallas_call(functools.partial(kernel, (ndet, nblk, nsub, spans, lanes,...]
    all_to_all x3 -> x0, starting transfers between devices: 14.8 us -> none  [the longest x1 6.48 us: on_device(): lax.all_to_all(tod, 'det', split_axis=1, concat_axis=0, tiled=True)]
    all_to_all x3 -> x0, waiting for transfers between devices: 9.42 us -> none  [the longest x1 4.93 us: on_device(): lax.all_to_all(tod, 'det', split_axis=1, concat_axis=0, tiled=True)]
    unnamed x1 -> x0, blocking collectives: 8.57 us -> none
    dot_general x9 -> x0, matrix products: 6.57 us -> none  [the longest x8 6.42 us: bin_tile(): lax.dot_general(stacked, low_hot, (((0,), (0,)), ((), ())), preferred_ele...]
    unnamed x12 -> x10, local copies, waits for them, and re-layouts: 2.17 us -> 3.92 us
    mul x8 -> x0, other arithmetic: 0.88 us -> none  [bin_tile(): first = tile_values[..., None] * high_hot]
    reduce_sum x2 -> x0, other arithmetic: 0.77 us -> none  [the longest x1 0.67 us: on_device(): total = jnp.sum(weight)]
  transfers between devices with their start and end apart: 3 -> 0, of which waited for: 2 -> 0; matrix products, arithmetic and copies ran while one was open for 25% -> 0% of each run, Pallas kernels for 0% -> 0%
where the time goes in v1:
time: 25.9 us; the launch traced here: 25.6 us
  Pallas kernels  21.1 us (81%)
  local copies, waits for them, and re-layouts  3.92 us (15%)
  between operations  0.66 us (3%)
    pallas_call x1, Pallas kernels, on_device(): pl.pallas_call(functools.partial(kernel, (ndet, nblk, nsub, spans, lanes,...  21.1 us
    unnamed x10, local copies, waits for them, and re-layouts  3.92 us

profile of v1, /device:TPU:0, one launch (start us, length us, event | category | flops | bytes accessed | tf_op | source)
XLA Modules:
  0.0 25.6 jit_solution(15408381403664942689)
XLA Ops:
  0.6 0.0 copy-start.2
  0.6 0.7 %copy-done.2 = s32[4,2]{0,1:T(2,128)S(1)} copy-done((s32[4,2]{0,1:T(2,128)S(1)}, s32[4,2]{0,1:T(2,128)}, u32[]{:S(2)}) %copy-start.2) | copy-done | bytes 56
  1.3 0.7 %copy.8.span_block_ref = s32[4,2]{1,0:T(4,128)} copy(s32[4,2]{0,1:T(2,128)S(1)} %copy-done.2) | data formatting | bytes 64 | tf_op args[2]
  2.0 21.1 %shard_map.76 = (f32[4,384]{1,0:T(4,128)}, f32[4,384]{1,0:T(4,128)}, f32[4,384]{1,0:T(4,128)}) custom-call(f32[32,4,256]{2,1,0:T(4,128)} %tod_hbm.1, s32[256,128]{1,0:T(8,128)} %bitcast.2, s32[1,128]{1,0:T(1,128)} %bitcast.3, f32[8]{0:T(128)} %class_weight_ref.1, s32[4,2]{1,0:T(4,128)} %copy.8.span_block_ref), custom_call_target="tpu_custom_call" | custom-call | tf_op jit(solution)/shard_map/pallas_call | solution.py:304
  23.0 0.0 copy-start.1
  23.0 1.3 %copy.12 = f32[4,384]{1,0:T(4,128)} copy(f32[4,384]{1,0:T(4,128)} %get-tuple-element.6) | data formatting | bytes 12288
  24.3 0.0 copy-done.1
  24.3 0.0 copy-start
  24.3 0.6 %copy.13 = f32[4,384]{1,0:T(4,128)} copy(f32[4,384]{1,0:T(4,128)S(1)} %copy-done.1) | data formatting | bytes 12288
  24.9 0.1 copy-done
  25.0 0.6 %copy.14 = f32[4,384]{1,0:T(4,128)} copy(f32[4,384]{1,0:T(4,128)S(1)} %copy-done) | data formatting | bytes 12288
Async XLA Ops:
  0.6 0.7 %copy-start.2 = (s32[4,2]{0,1:T(2,128)S(1)}, s32[4,2]{0,1:T(2,128)}, u32[]{:S(2)}) copy-start(s32[4,2]{0,1:T(2,128)} %param.7) | copy-start | bytes 100
  23.0 1.3 %copy-start.1 = (f32[4,384]{1,0:T(4,128)S(1)}, f32[4,384]{1,0:T(4,128)}, u32[]{:S(2)}) copy-start(f32[4,384]{1,0:T(4,128)} %get-tuple-element.7) | copy-start | bytes 18436
  24.3 0.7 %copy-start = (f32[4,384]{1,0:T(4,128)S(1)}, f32[4,384]{1,0:T(4,128)}, u32[]{:S(2)}) copy-start(f32[4,384]{1,0:T(4,128)} %get-tuple-element.8) | copy-start | bytes 18436

commit v2 on v1

--- a/solution.py
+++ b/solution.py
@@ -22,9 +22,7 @@
     class_ref,
     class_weight_ref,
     span_block_ref,
-    signal_ref,
-    weight_ref,
-    hits_ref,
+    out_ref,
     tod_in,
     pix_in,
     stage,
@@ -169,7 +167,7 @@
     sums = lax.fori_loop(0, detectors // chunk, early_step, start)
     label_row = lax.broadcasted_iota(jnp.int32, (TILE, SPAN), 0) == 2 * rows
     for span in range(spans):
-        label = span_block_ref[det, span].astype(jnp.float32)
+        label = span_block_ref[span, det].astype(jnp.float32)
         for p in range(peers):
             tile = sums[span][p * TILE : (p + 1) * TILE]
             early_out[p, span] = jnp.where(label_row, label, tile)
@@ -265,8 +263,8 @@
     for b in range(BLK_OWN):
         for r in range(rows):
             at = slice(r * lanes, (r + 1) * lanes)
-            weight_ref[b : b + 1, at] = acc[b][r : r + 1, :lanes]
-            hits_ref[b : b + 1, at] = acc[b][rows + r : rows + r + 1, :lanes]
+            out_ref[1, b : b + 1, at] = acc[b][r : r + 1, :lanes]
+            out_ref[2, b : b + 1, at] = acc[b][rows + r : rows + r + 1, :lanes]
 
     pltpu.make_async_copy(late_in.at[pl.ds(0, remote)], late_in.at[pl.ds(0, remote)], late_recv).wait()
     acc = over_slots(gather_late)
@@ -275,7 +273,7 @@
             line = acc[b][r : r + 1]
             for span in range(1, spans):
                 line = line + acc[b][span * rows + r : span * rows + r + 1]
-            signal_ref[b : b + 1, r * lanes : (r + 1) * lanes] = line[:, :lanes]
+            out_ref[0, b : b + 1, r * lanes : (r + 1) * lanes] = line[:, :lanes]
 
     pltpu.make_async_copy(tod_gone, tod_all.at[pl.ds(0, ndet - 1)], tod_send).wait()
     pltpu.make_async_copy(early_in.at[pl.ds(0, remote)], early_in.at[pl.ds(0, remote)], early_send).wait()
@@ -295,17 +293,16 @@
     assert segments == ndet and detectors == ndet * mine
     assert TILE % spans == 0 and rows * spans <= TILE and 2 * rows < TILE
     flat = (detectors * spans, SPAN)
-    out = jax.ShapeDtypeStruct((BLK_OWN, width), jnp.float32)
     vmem = pl.BlockSpec(memory_space=pltpu.VMEM)
     smem = pl.BlockSpec(memory_space=pltpu.SMEM)
     hbm = pl.BlockSpec(memory_space=pl.ANY)
     f32 = jnp.float32
     dma = pltpu.SemaphoreType.DMA
-    return pl.pallas_call(
+    out = pl.pallas_call(
         functools.partial(kernel, (ndet, nblk, nsub, spans, lanes, rows)),
-        out_shape=(out, out, out),
+        out_shape=pltpu.VMEM((3, BLK_OWN, width), f32),
         in_specs=[hbm, hbm, vmem, smem, smem],
-        out_specs=(vmem, vmem, vmem),
+        out_specs=vmem,
         scratch_shapes=[
             pltpu.VMEM(tod.shape, f32),
             pltpu.VMEM(flat, jnp.int32),
@@ -333,8 +330,9 @@
         pixels.reshape(flat),
         weight_class.reshape(1, detectors),
         class_weight,
-        span_block,
+        span_block.T,
     )
+    return (out[0], out[1], out[2])
 
 
 def solution(mesh):

time: 25.9 us -> 21.9 us (0.85)
  local copies, waits for them, and re-layouts: 3.92 us -> 0.6 us
  Pallas kernels: 21.1 us -> 20.5 us
    unnamed x10 -> x0, local copies, waits for them, and re-layouts: 3.92 us -> none
    squeeze x0 -> x1, local copies, waits for them, and re-layouts: none -> 0.6 us  [on_device(): return (out[0], out[1], out[2])]
    pallas_call x1, Pallas kernels: 21.1 us -> 20.5 us  [on_device(): pl.pallas_call(functools.partial(kernel, (ndet, nblk, nsub, spans, lanes,...]
where the time goes in v2:
time: 21.9 us; the launch traced here: 21.7 us
  Pallas kernels  20.5 us (94%)
  between operations  0.64 us (3%)
  local copies, waits for them, and re-layouts  0.6 us (3%)
    pallas_call x1, Pallas kernels, on_device(): pl.pallas_call(functools.partial(kernel, (ndet, nblk, nsub, spans, lanes,...  20.5 us
    squeeze x1, local copies, waits for them, and re-layouts, on_device(): return (out[0], out[1], out[2])  0.6 us

profile of v2, /device:TPU:0, one launch (start us, length us, event | category | flops | bytes accessed | tf_op | source)
XLA Modules:
  0.0 21.7 jit_solution(11740478675664121051)
XLA Ops:
  0.6 20.5 %shard_map.76 = f32[3,4,384]{2,1,0:T(4,128)S(1)} custom-call(f32[32,4,256]{2,1,0:T(4,128)} %tod_hbm.1, s32[256,128]{1,0:T(8,128)} %bitcast.9, s32[1,128]{1,0:T(1,128)} %bitcast.11, f32[8]{0:T(128)} %class_weight_ref.1, s32[2,4]{1,0:T(2,128)} %bitcast.10), custom_call_target="tpu_custom_call" | custom-call | tf_op jit(solution)/shard_map/pallas_call | solution.py:301
  21.1 0.6 %slice_bitcast_fusion = (f32[4,384]{1,0:T(4,128)}, f32[4,384]{1,0:T(4,128)}, f32[4,384]{1,0:T(4,128)}) fusion(f32[3,4,384]{2,1,0:T(4,128)S(1)} %shard_map.76), kind=kLoop, calls=%fused_computation | loop fusion | bytes 36864 | tf_op jit(solution)/shard_map/squeeze | solution.py:335

commit v3 on v2

--- a/solution.py
+++ b/solution.py
@@ -19,16 +19,21 @@
     sizes,
     tod_hbm,
     pix_hbm,
+    class_hbm,
+    class_weight_hbm,
+    span_block_hbm,
+    out_ref,
     class_ref,
     class_weight_ref,
     span_block_ref,
-    out_ref,
     tod_in,
     pix_in,
     stage,
     tod_all,
     high_ref,
     low_ref,
+    fine_high_ref,
+    fine_low_ref,
     weight_rows,
     value_ref,
     early_out,
@@ -42,20 +47,17 @@
     early_recv,
     late_send,
     late_recv,
+    passed,
 ):
     ndet, nblk, nsub, spans, lanes, rows = sizes
     peers = ndet * nsub
     total_peers = peers * nblk
     mine = tod_hbm.shape[0]
     detectors = ndet * mine
-    classes = class_weight_ref.shape[0]
+    classes = class_weight_hbm.shape[0]
     det = lax.axis_index("det")
     blk = lax.axis_index("blk")
     sub = lax.axis_index("sub")
-    load_tod = pltpu.make_async_copy(tod_hbm, tod_in, load_sem.at[0])
-    load_pix = pltpu.make_async_copy(pix_hbm, pix_in, load_sem.at[1])
-    load_tod.start()
-    load_pix.start()
     others = [
         (db, dd, ds)
         for dd in range(ndet)
@@ -73,15 +75,28 @@
         }
 
     barrier = pltpu.get_barrier_semaphore()
-    for offset in others:
+    plane = [offset for offset in others if offset[1] == 0]
+    column = [offset for offset in others if offset[0] == 0 and offset[2] == 0]
+    for offset in plane + column:
         pl.semaphore_signal(barrier, inc=1, device_id=target(offset), device_id_type=MESH)
 
+    sources = (tod_hbm, pix_hbm, class_hbm, class_weight_hbm, span_block_hbm)
+    landings = (tod_in, pix_in, class_ref, class_weight_ref, span_block_ref)
+    loads = [
+        pltpu.make_async_copy(source, landing, load_sem.at[n])
+        for n, (source, landing) in enumerate(zip(sources, landings))
+    ]
+    for load in loads:
+        load.start()
+
     part = mine * spans
-    load_tod.wait()
+    loads[0].wait()
     for seg in range(ndet):
         for span in range(spans):
             stage[seg, pl.ds(span, mine, spans), :] = tod_in[:, seg, span * SPAN : (span + 1) * SPAN]
-    pl.semaphore_wait(barrier, len(others))
+    pl.semaphore_wait(barrier, len(plane + column))
+    for offset in plane:
+        pl.semaphore_signal(passed, inc=1, device_id=target(offset), device_id_type=MESH)
     for step in range(1, ndet):
         seg = lax.rem(det + step, ndet)
         pltpu.make_async_remote_copy(
@@ -94,6 +109,8 @@
         ).start()
     tod_all[det] = stage[det]
 
+    loads[2].wait()
+    loads[3].wait()
     picked = jnp.zeros((1, detectors), jnp.float32)
     for c in range(classes):
         picked = jnp.where(class_ref[...] == c, class_weight_ref[c], picked)
@@ -102,13 +119,20 @@
     for span in range(spans):
         weight_rows[pl.ds(span, detectors, spans), :] = turned
 
-    load_pix.wait()
+    loads[1].wait()
     pixel = pix_in[...].astype(jnp.float32)
     high = jnp.floor((pixel + 0.5) * (1.0 / lanes))
     high_ref[...] = high
-    low_ref[...] = pixel - high * lanes
+    low = pixel - high * lanes
+    low_ref[...] = low
+    upper = jnp.where(low >= lanes // 2, 1.0, 0.0)
+    fine_high_ref[...] = 2.0 * high + upper
+    fine_low_ref[...] = low - upper * (lanes // 2)
 
     height = peers * TILE
+    fine = lanes // 2
+    fine_rows = 2 * rows
+    field = SPAN // spans
     low_tiles = -(-lanes // PACK)
 
     def iota(tile):
@@ -119,17 +143,17 @@
 
     low_ids = [to_low(iota(t)) for t in range(SPAN // PACK)]
     early_ids = []
-    late_ids = [[] for _ in range(spans)]
+    late_ids = []
     for t in range(height // PACK):
         row = iota(t)
         peer = row // TILE
         within = row % TILE
         kind = jnp.where(within < rows, within, within - rows)
         early_ids.append(to_low(jnp.where(within < 2 * rows, peer * rows + kind, -1)))
-        for span in range(spans):
-            inner = within - span * rows
-            valid = jnp.logical_and(inner >= 0, inner < rows)
-            late_ids[span].append(to_low(jnp.where(valid, peer * rows + inner, -1)))
+    for t in range(height // PACK):
+        row = iota(t)
+        within = row % TILE
+        late_ids.append(to_low(jnp.where(within < fine_rows, row // TILE * fine_rows + within, -1)))
     is_weight = to_low(jnp.where(iota(0) % TILE < rows, 1, 0)) > 0.5
     one = jnp.ones((PACK, SPAN), jnp.bfloat16)
     zero = jnp.zeros((PACK, SPAN), jnp.bfloat16)
@@ -140,7 +164,7 @@
     def hot(ids, where, filled):
         return jnp.concatenate([jnp.where(i == where, filled, zero) for i in ids], axis=0)
 
-    chunk = 8
+    chunk = min(64, detectors)
 
     def contract(left, right):
         return lax.dot_general(
@@ -165,6 +189,7 @@
 
     start = tuple(jnp.zeros((height, SPAN), jnp.float32) for _ in range(spans))
     sums = lax.fori_loop(0, detectors // chunk, early_step, start)
+    loads[4].wait()
     label_row = lax.broadcasted_iota(jnp.int32, (TILE, SPAN), 0) == 2 * rows
     for span in range(spans):
         label = span_block_ref[span, det].astype(jnp.float32)
@@ -189,9 +214,11 @@
     own_place = det * nsub + sub
     remote = len(others)
 
+    pl.semaphore_wait(passed, len(plane))
+    send(early_out, early_in, early_send, early_recv)
+
     tod_gone = stage.at[pl.ds(0, ndet - 1)]
     pltpu.make_async_copy(tod_gone, tod_all.at[pl.ds(0, ndet - 1)], tod_recv).wait()
-    send(early_out, early_in, early_send, early_recv)
 
     period = TILE
     folded = jnp.zeros((period, SPAN), jnp.float32)
@@ -209,20 +236,23 @@
         repeated = jnp.concatenate([common] * (part // period), axis=0)
         value_ref[piece] = weight_rows[piece] * (tod_all[q] - repeated)
 
-    def late_step(i, total_sum):
+    def late_step(i, sums):
         base = pl.multiple_of(i * chunk * spans, TILE)
+        new = []
         for span in range(spans):
             left, right = [], []
             for d in range(chunk):
                 r = base + d * spans + span
-                right.append(hot(low_ids, spread(low_ref, r), one))
-                left.append(hot(late_ids[span], spread(high_ref, r), spread(value_ref, r)))
-            total_sum = total_sum + contract(left, right)
-        return total_sum
-
-    late = lax.fori_loop(0, detectors // chunk, late_step, jnp.zeros((height, SPAN), jnp.float32))
+                right.append(hot(low_ids[: field // PACK], spread(fine_low_ref, r), one))
+                left.append(hot(late_ids, spread(fine_high_ref, r), spread(value_ref, r)))
+            new.append(sums[span] + contract(left, right))
+        return tuple(new)
+
+    start = tuple(jnp.zeros((height, field), jnp.float32) for _ in range(spans))
+    late = lax.fori_loop(0, detectors // chunk, late_step, start)
     for p in range(peers):
-        late_out[p] = late[p * TILE : (p + 1) * TILE]
+        tiles = [late[span][p * TILE : (p + 1) * TILE] for span in range(spans)]
+        late_out[p] = jnp.concatenate(tiles, axis=1)
     send(late_out, late_in, late_send, late_recv)
     late_in[remote] = late_out[own_place]
     early_in[remote] = early_out[own_place]
@@ -239,13 +269,13 @@
                 acc[b] = acc[b] + jnp.where(label == first + b, tile, 0.0)
         return tuple(acc)
 
-    within = lax.broadcasted_iota(jnp.int32, (TILE, SPAN), 0)
+    lane = lax.broadcasted_iota(jnp.int32, (TILE, SPAN), 1)
 
     def gather_late(n, acc):
         label = jnp.broadcast_to(early_in[n, 0, pl.ds(2 * rows, 1), :], (TILE, SPAN))
         for span in range(1, spans):
             other = jnp.broadcast_to(early_in[n, span, pl.ds(2 * rows, 1), :], (TILE, SPAN))
-            label = jnp.where(within < span * rows, label, other)
+            label = jnp.where(lane < span * field, label, other)
         tile = late_in[n]
         return tuple(
             acc[b] + jnp.where(label == first + b, tile, 0.0) for b in range(BLK_OWN)
@@ -269,11 +299,14 @@
     pltpu.make_async_copy(late_in.at[pl.ds(0, remote)], late_in.at[pl.ds(0, remote)], late_recv).wait()
     acc = over_slots(gather_late)
     for b in range(BLK_OWN):
-        for r in range(rows):
-            line = acc[b][r : r + 1]
-            for span in range(1, spans):
-                line = line + acc[b][span * rows + r : span * rows + r + 1]
-            out_ref[0, b : b + 1, r * lanes : (r + 1) * lanes] = line[:, :lanes]
+        whole = acc[b]
+        for span in range(1, spans):
+            whole = whole + pltpu.roll(acc[b], span * field, 1)
+        for r in range(fine_rows):
+            skip = r * fine % SPAN // field * field
+            skip = skip if skip + fine <= SPAN else 0
+            line = whole[r : r + 1, skip : skip + fine]
+            out_ref[0, b : b + 1, r * fine : (r + 1) * fine] = line
 
     pltpu.make_async_copy(tod_gone, tod_all.at[pl.ds(0, ndet - 1)], tod_send).wait()
     pltpu.make_async_copy(early_in.at[pl.ds(0, remote)], early_in.at[pl.ds(0, remote)], early_send).wait()
@@ -291,19 +324,21 @@
     lanes = next(n for n in range(SPAN, 0, -1) if width % n == 0)
     rows = width // lanes
     assert segments == ndet and detectors == ndet * mine
-    assert TILE % spans == 0 and rows * spans <= TILE and 2 * rows < TILE
+    assert TILE % spans == 0 and 2 * rows < TILE and lanes % 2 == 0 and lanes // 2 <= SPAN // spans
     flat = (detectors * spans, SPAN)
     vmem = pl.BlockSpec(memory_space=pltpu.VMEM)
-    smem = pl.BlockSpec(memory_space=pltpu.SMEM)
     hbm = pl.BlockSpec(memory_space=pl.ANY)
     f32 = jnp.float32
     dma = pltpu.SemaphoreType.DMA
     out = pl.pallas_call(
         functools.partial(kernel, (ndet, nblk, nsub, spans, lanes, rows)),
         out_shape=pltpu.VMEM((3, BLK_OWN, width), f32),
-        in_specs=[hbm, hbm, vmem, smem, smem],
+        in_specs=[hbm] * 5,
         out_specs=vmem,
         scratch_shapes=[
+            pltpu.VMEM((1, detectors), jnp.int32),
+            pltpu.SMEM(class_weight.shape, f32),
+            pltpu.SMEM((spans, segments), jnp.int32),
             pltpu.VMEM(tod.shape, f32),
             pltpu.VMEM(flat, jnp.int32),
             pltpu.VMEM((ndet, mine * spans, SPAN), f32),
@@ -312,17 +347,20 @@
             pltpu.VMEM(flat, f32),
             pltpu.VMEM(flat, f32),
             pltpu.VMEM(flat, f32),
+            pltpu.VMEM(flat, f32),
+            pltpu.VMEM(flat, f32),
             pltpu.VMEM((peers, spans, TILE, SPAN), f32),
             pltpu.VMEM((slots, spans, TILE, SPAN), f32),
             pltpu.VMEM((peers, TILE, SPAN), f32),
             pltpu.VMEM((slots, TILE, SPAN), f32),
-            dma((2,)),
-            dma,
-            dma,
-            dma,
-            dma,
-            dma,
-            dma,
+            dma((5,)),
+            dma,
+            dma,
+            dma,
+            dma,
+            dma,
+            dma,
+            pltpu.SemaphoreType.REGULAR,
         ],
         compiler_params=pltpu.CompilerParams(collective_id=0, has_side_effects=True),
     )(

time: 21.9 us -> 17.6 us (0.80)
  Pallas kernels: 20.5 us -> 16.2 us
    pallas_call x1, Pallas kernels: 20.5 us -> 16.2 us  [on_device(): pl.pallas_call(functools.partial(kernel, (ndet, nblk, nsub, spans, lanes,...]
where the time goes in v3:
time: 17.6 us; the launch traced here: 17.4 us
  Pallas kernels  16.2 us (92%)
  between operations  0.64 us (4%)
  local copies, waits for them, and re-layouts  0.6 us (3%)
    pallas_call x1, Pallas kernels, on_device(): pl.pallas_call(functools.partial(kernel, (ndet, nblk, nsub, spans, lanes,...  16.2 us
    squeeze x1, local copies, waits for them, and re-layouts, on_device(): return (out[0], out[1], out[2])  0.6 us

profile of v3, /device:TPU:0, one launch (start us, length us, event | category | flops | bytes accessed | tf_op | source)
XLA Modules:
  0.0 17.4 jit_solution(12605220464399961364)
XLA Ops:
  0.6 16.2 %shard_map.76 = f32[3,4,384]{2,1,0:T(4,128)S(1)} custom-call(f32[32,4,256]{2,1,0:T(4,128)} %tod_hbm.1, s32[256,128]{1,0:T(8,128)} %bitcast.9, s32[1,128]{1,0:T(1,128)} %bitcast.11, f32[8]{0:T(128)} %class_weight_hbm.1, s32[2,4]{1,0:T(2,128)} %bitcast.10), custom_call_target="tpu_custom_call" | custom-call | tf_op jit(solution)/shard_map/pallas_call | solution.py:333
  16.8 0.6 %slice_bitcast_fusion = (f32[4,384]{1,0:T(4,128)}, f32[4,384]{1,0:T(4,128)}, f32[4,384]{1,0:T(4,128)}) fusion(f32[3,4,384]{2,1,0:T(4,128)S(1)} %shard_map.76), kind=kLoop, calls=%fused_computation | loop fusion | bytes 36864 | tf_op jit(solution)/shard_map/squeeze | solution.py:373

commit v4 on v3

--- a/solution.py
+++ b/solution.py
@@ -94,6 +94,27 @@
     for seg in range(ndet):
         for span in range(spans):
             stage[seg, pl.ds(span, mine, spans), :] = tod_in[:, seg, span * SPAN : (span + 1) * SPAN]
+
+    loads[2].wait()
+    loads[3].wait()
+    picked = jnp.zeros((1, detectors), jnp.float32)
+    for c in range(classes):
+        picked = jnp.where(class_ref[...] == c, class_weight_ref[c], picked)
+    total = jnp.sum(picked, axis=1, keepdims=True)
+    turned = jnp.transpose(jnp.broadcast_to(picked, (SPAN, detectors)))
+    for span in range(spans):
+        weight_rows[pl.ds(span, detectors, spans), :] = turned
+
+    loads[1].wait()
+    pixel = pix_in[...].astype(jnp.float32)
+    high = jnp.floor((pixel + 0.5) * (1.0 / lanes))
+    high_ref[...] = high
+    low = pixel - high * lanes
+    low_ref[...] = low
+    upper = jnp.where(low >= lanes // 2, 1.0, 0.0)
+    fine_high_ref[...] = 2.0 * high + upper
+    fine_low_ref[...] = low - upper * (lanes // 2)
+
     pl.semaphore_wait(barrier, len(plane + column))
     for offset in plane:
         pl.semaphore_signal(passed, inc=1, device_id=target(offset), device_id_type=MESH)
@@ -108,27 +129,6 @@
             device_id_type=MESH,
         ).start()
     tod_all[det] = stage[det]
-
-    loads[2].wait()
-    loads[3].wait()
-    picked = jnp.zeros((1, detectors), jnp.float32)
-    for c in range(classes):
-        picked = jnp.where(class_ref[...] == c, class_weight_ref[c], picked)
-    total = jnp.sum(picked, axis=1, keepdims=True)
-    turned = jnp.transpose(jnp.broadcast_to(picked, (SPAN, detectors)))
-    for span in range(spans):
-        weight_rows[pl.ds(span, detectors, spans), :] = turned
-
-    loads[1].wait()
-    pixel = pix_in[...].astype(jnp.float32)
-    high = jnp.floor((pixel + 0.5) * (1.0 / lanes))
-    high_ref[...] = high
-    low = pixel - high * lanes
-    low_ref[...] = low
-    upper = jnp.where(low >= lanes // 2, 1.0, 0.0)
-    fine_high_ref[...] = 2.0 * high + upper
-    fine_low_ref[...] = low - upper * (lanes // 2)
-
     height = peers * TILE
     fine = lanes // 2
     fine_rows = 2 * rows

time: 17.6 us -> 17.5 us (level)
  no operation moved by 1% of the time
where the time goes in v4:
time: 17.5 us; the launch traced here: 17.4 us
  Pallas kernels  16.1 us (92%)
  between operations  0.64 us (4%)
  local copies, waits for them, and re-layouts  0.6 us (3%)
    pallas_call x1, Pallas kernels, on_device(): pl.pallas_call(functools.partial(kernel, (ndet, nblk, nsub, spans, lanes,...  16.1 us
    squeeze x1, local copies, waits for them, and re-layouts, on_device(): return (out[0], out[1], out[2])  0.6 us

profile of v4, /device:TPU:0, one launch (start us, length us, event | category | flops | bytes accessed | tf_op | source)
XLA Modules:
  0.0 17.4 jit_solution(2608787938999089473)
XLA Ops:
  0.6 16.1 %shard_map.76 = f32[3,4,384]{2,1,0:T(4,128)S(1)} custom-call(f32[32,4,256]{2,1,0:T(4,128)} %tod_hbm.1, s32[256,128]{1,0:T(8,128)} %bitcast.9, s32[1,128]{1,0:T(1,128)} %bitcast.11, f32[8]{0:T(128)} %class_weight_hbm.1, s32[2,4]{1,0:T(2,128)} %bitcast.10), custom_call_target="tpu_custom_call" | custom-call | tf_op jit(solution)/shard_map/pallas_call | solution.py:333
  16.8 0.6 %slice_bitcast_fusion = (f32[4,384]{1,0:T(4,128)}, f32[4,384]{1,0:T(4,128)}, f32[4,384]{1,0:T(4,128)}) fusion(f32[3,4,384]{2,1,0:T(4,128)S(1)} %shard_map.76), kind=kLoop, calls=%fused_computation | loop fusion | bytes 36864 | tf_op jit(solution)/shard_map/squeeze | solution.py:373
